TPU v7x, 32 devices: a whole 2x2x4 slice. The times are simulated.
32 devices in a mesh: groups: 2 (over x), freq: 16 (over z, y, core).
Axes of the slice: x: 2, y: 2, z: 4, core: 2. Of those that a mesh axis runs over, the one named last changes fastest.
Arguments:
- traces: bfloat16 [1024, 2048, 32], P('freq', None, 'groups'), parts along dimension 2, may hold values from -6 to 6
- freq_index: int32 [16], replicated, may hold values from 1 to 511
- block_map: int32 [64, 64], replicated, may hold values 0 or 1
- green_rec: bfloat16 [16, 2, 2048, 1536], P('freq', None, None, 'groups'), parts along dimension 3, may hold values from -0.1875 to 0.1875
- green_src: bfloat16 [16, 2, 16, 1536], P('freq', None, None, 'groups'), parts along dimension 3, may hold values from -0.25 to 0.25
Outputs:
- image: float32 [1536], P(('groups', 'freq')), parts along dimension 0
There are 2 independent parts, one for each index of `groups`. A program takes and returns all parts, laid end to end along the dimension named above; an argument that names none is the same for every part. Nothing has to cross between parts.
Inputs may be any that keep to these rules, and one draw needn't show every extreme that they name: `freq_index`: frequency bins; they may repeat. `block_map`: 1 where a receiver block lies in an image tile's aperture.
All inputs are finite; a program needn't handle non-finite values.
Results may differ from a plain program's by a relative error of at most 0.0038.
Values may be sent and summed in bfloat16 or wider, within the bound.
No kernel may reach another device: no remote copies, remote signals or barrier semaphores. Data moves between devices by JAX's collectives and lax.ppermute only.
A program may use at most 64 MiB of HBM per device.

v0:
```python
import math
import jax
import jax.numpy as jnp
from jax import lax
from jax.sharding import PartitionSpec as P


def dft_table(freq_index, length):
    sample_index = jnp.arange(length, dtype=jnp.int32)
    phases = freq_index[:, None] * sample_index[None, :] % length
    angles = phases.astype(jnp.float32) * jnp.float32(2.0 * math.pi / length)
    stacked = jnp.stack((jnp.cos(angles), -jnp.sin(angles)), axis=1)
    return stacked.reshape(freq_index.shape[0] * 2, length).astype(jnp.bfloat16)


def expand_map(block_map, receivers, points):
    row_span = receivers // block_map.shape[0]
    col_span = points // block_map.shape[1]
    return jnp.repeat(jnp.repeat(block_map, row_span, axis=0), col_span, axis=1).astype(
        jnp.bfloat16
    )


def transform(cos_table, records, length):
    spectrum = jnp.dot(cos_table, records.reshape(length, -1), preferred_element_type=jnp.float32)
    return (spectrum * (1.0 / math.sqrt(length))).astype(jnp.bfloat16)


def back_project(spectra, masked):
    swapped = jnp.stack((spectra[:, 1], -spectra[:, 0]), axis=1)
    blocks = jnp.stack((spectra, swapped), axis=1)
    return jnp.einsum("fcrx,focrs->fosx", masked, blocks, preferred_element_type=jnp.float32)


def body(traces, freq_index, block_map, green_rec, green_src):
    shards = lax.axis_size("freq")
    length = traces.shape[0] * shards
    receivers = traces.shape[1]
    shots = traces.shape[2]
    freqs = freq_index.shape[0]
    cos_table = dft_table(freq_index, length)
    masked = green_rec * expand_map(block_map, receivers, green_rec.shape[3])[None, None]
    regrouped = lax.all_to_all(traces, "freq", split_axis=2, concat_axis=0, tiled=True)
    spectrum = transform(cos_table, regrouped, length).reshape(freqs, 2, receivers, shots // shards)
    gathered = lax.all_to_all(spectrum, "freq", split_axis=0, concat_axis=3, tiled=True)
    back_field = back_project(gathered, masked)
    partial_image = jnp.sum(green_src.astype(jnp.float32) * back_field, axis=(0, 1, 2))
    return lax.psum_scatter(partial_image, "freq", scatter_dimension=0, tiled=True)


def solution(mesh):
    in_specs = (
        P("freq", None, "groups"),
        P(),
        P(),
        P("freq", None, None, "groups"),
        P("freq", None, None, "groups"),
    )
    out_specs = P(("groups", "freq"))
    return jax.shard_map(body, mesh=mesh, in_specs=in_specs, out_specs=out_specs, check_vma=False)
```

profile of v0, /device:TPU:0, one launch (start us, length us, event | category | flops | bytes accessed | tf_op | source)
XLA Modules:
  0.0 166.9 jit_solution(11297971137079490773)
XLA Ops:
  0.0 6.4 %copy.26 = bf16[64,2048,16]{1,0,2:T(8,128)(2,1)} copy(bf16[64,2048,16]{1,2,0:T(8,128)(2,1)} %param.5) | data formatting | bytes 8388608 | tf_op args[0]
  6.4 0.0 copy-start.2
  6.5 7.6 %all-to-all-start = ((bf16[64,2048,16]{1,0,2:T(8,128)(2,1)}), bf16[64,2048,16]{1,0,2:T(8,128)(2,1)}, u32[]{:S(2)}, u32[]{:S(2)}) async-start(bf16[64,2048,16]{1,0,2:T(8,128)(2,1)} %copy.26), calls=%async_computation | async-start | bytes 8388608 | tf_op jit(solution)/shard_map/all_to_all | solution.py:43
  14.1 0.0 copy-done.2
  14.1 0.0 copy-start.1
  14.1 0.3 cosine_convert_fusion
  14.4 0.1 copy.25
  14.6 77.0 %all-to-all-done = bf16[64,2048,16]{1,0,2:T(8,128)(2,1)} async-done(((bf16[64,2048,16]{1,0,2:T(8,128)(2,1)}), bf16[64,2048,16]{1,0,2:T(8,128)(2,1)}, u32[]{:S(2)}, u32[]{:S(2)}) %all-to-all-start) | async-done | bytes 4194336 | tf_op jit(solution)/shard_map/all_to_all | solution.py:43
  91.6 3.0 %fusion.4 = bf16[32,2048]{1,0:T(8,128)(2,1)S(1)} fusion(bf16[32,1024]{1,0:T(8,128)(2,1)S(1)} %convert_element_type.47, bf16[1024,2048]{1,0:T(8,128)(2,1)} %bitcast.2), kind=kOutput, calls=%fused_computation.5 | convolution fusion | flops 134348800 | bytes 4390912 | tf_op jit(solution)/shard_map/dot_general | solution.py:25
  94.6 0.8 reshape.132
  95.4 19.6 %all-to-all-start.1 = ((bf16[16,2,2048,1]{2,1,3,0:T(2,128)(2,1)}), bf16[16,2,2048,1]{2,1,3,0:T(2,128)(2,1)S(1)}, u32[]{:S(2)}, u32[]{:S(2)}) async-start(bf16[16,2,2048,1]{2,1,3,0:T(2,128)(2,1)} %bitcast.3), calls=%async_computation.1 | async-start | bytes 262144 | tf_op jit(solution)/shard_map/all_to_all | solution.py:45
  115.0 0.0 copy-done.1
  115.1 0.1 broadcast_in_dim.4
  115.1 0.2 copy.29
  115.3 2.5 %broadcast_in_dim.10 = bf16[2048,64,12]{0,2,1:T(8,128)(2,1)} broadcast(bf16[2048,64]{0,1:T(8,128)(2,1)S(1)} %copy.29), dimensions={0,1} | broadcast | bytes 3407872 | tf_op jit(solution)/shard_map/broadcast_in_dim | solution.py:19
  117.8 6.2 %convert_element_type.51 = bf16[2048,768]{0,1:T(8,128)(2,1)} reshape(bf16[2048,64,12]{0,2,1:T(8,128)(2,1)} %broadcast_in_dim.10) | data formatting | bytes 6291456 | tf_op jit(solution)/shard_map/convert_element_type | solution.py:19
  124.0 0.0 copy-start.3
  124.0 0.0 copy-start
  124.0 3.2 %copy.30 = bf16[2048,768]{1,0:T(8,128)(2,1)S(1)} copy(bf16[2048,768]{0,1:T(8,128)(2,1)} %convert_element_type.51) | data formatting | bytes 6291456 | tf_op jit(solution)/shard_map/convert_element_type | solution.py:19
  127.2 0.0 copy-done.3
  127.2 0.6 dynamic-slice
  128.4 0.0 all-to-all-done.1
  128.5 0.0 copy-done
  128.5 4.0 %fusion.11 = f32[768]{0:T(1024)S(1)} fusion(bf16[1,2,2048,768]{3,2,1,0:T(8,128)(2,1)} %param.8, bf16[2048,768]{1,0:T(8,128)(2,1)S(1)} %copy.30, bf16[1,1,2,2048,16]{3,4,2,1,0:T(8,128)(2,1)S(1)} %maximum_bitcast_fusion.2, bf16[1,1,2,2048,16]{3,4,2,1,0:T(8,128)(2,1)S(1)} %bitcast.47, bf16[1,2,16,768]{3,2,1,0:T(8,128)(2,1)S(1)} %copy-done), kind=kOutput, calls=%fused_computation.8 | convolution fusion | flops 204676352 | bytes 9751552 | tf_op jit(solution)/shard_map/fcrx,focrs->fosx/dot_general | solution.py:32
  132.5 33.8 %all-reduce = f32[768]{0:T(1024)S(1)} all-reduce(f32[768]{0:T(1024)S(1)} %fusion.11), channel_id=2, replica_groups=mesh['groups'=2,'freq'=16] {'freq'}, use_global_device_ids=true, to_apply=%region_1.2.clone | all-reduce | flops 768 | bytes 6144
  166.3 0.6 dynamic-slice.1
  (6 shorter events, 0.1 us)
Async XLA Ops:
  6.4 7.6 %copy-start.2 = (s32[16]{0:T(128)S(1)}, s32[16]{0:T(128)}, u32[]{:S(2)}) copy-start(s32[16]{0:T(128)} %param.6) | copy-start | bytes 196
  6.5 85.1 %all-to-all-start = ((bf16[64,2048,16]{1,0,2:T(8,128)(2,1)}), bf16[64,2048,16]{1,0,2:T(8,128)(2,1)}, u32[]{:S(2)}, u32[]{:S(2)}) async-start(bf16[64,2048,16]{1,0,2:T(8,128)(2,1)} %copy.26), calls=%async_computation | async-start | bytes 8388608 | tf_op jit(solution)/shard_map/all_to_all | solution.py:43
  14.1 101.0 %copy-start.1 = (s32[64,64]{1,0:T(8,128)S(1)}, s32[64,64]{1,0:T(8,128)}, u32[]{:S(2)}) copy-start(s32[64,64]{1,0:T(8,128)} %param.7) | copy-start | bytes 49156
  95.4 33.1 %all-to-all-start.1 = ((bf16[16,2,2048,1]{2,1,3,0:T(2,128)(2,1)}), bf16[16,2,2048,1]{2,1,3,0:T(2,128)(2,1)S(1)}, u32[]{:S(2)}, u32[]{:S(2)}) async-start(bf16[16,2,2048,1]{2,1,3,0:T(2,128)(2,1)} %bitcast.3), calls=%async_computation.1 | async-start | bytes 262144 | tf_op jit(solution)/shard_map/all_to_all | solution.py:45
  124.0 3.2 %copy-start.3 = (u32[32]{0:T(128)S(1)}, u32[32]{0:T(128)}, u32[]{:S(2)}) copy-start(u32[32]{0:T(128)} %constant.25) | copy-start | bytes 388
  124.0 4.6 %copy-start = (bf16[1,2,16,768]{3,2,1,0:T(8,128)(2,1)S(1)}, bf16[1,2,16,768]{3,2,1,0:T(8,128)(2,1)}, u32[]{:S(2)}) copy-start(bf16[1,2,16,768]{3,2,1,0:T(8,128)(2,1)} %param.9) | copy-start | bytes 147460
where the time goes:
time: 168 us; the launch traced here: 167 us
  waiting for transfers between devices  77.1 us (46%)
  blocking collectives  33.8 us (20%)
  starting transfers between devices  27.2 us (16%)
  local copies, waits for them, and re-layouts  20.6 us (12%)
  matrix products  6.97 us (4%)
    all_to_all x1, waiting for transfers between devices, body(): lax.all_to_all(traces, 'freq', split_axis=2, concat_axis=0, tiled=True)  77 us
    unnamed x1, blocking collectives  33.8 us
    all_to_all x1, starting transfers between devices, body(): lax.all_to_all(spectrum, 'freq', split_axis=0, concat_axis=3, tiled=True)  19.6 us
    convert_element_type x3, local copies, waits for them, and re-layouts, expand_map(): jnp.repeat(jnp.repeat(block_map, row_span, axis=0), col_span, axis=1)  9.56 us
    unnamed x11, local copies, waits for them, and re-layouts  7.64 us
    all_to_all x1, starting transfers between devices, body(): lax.all_to_all(traces, 'freq', split_axis=2, concat_axis=0, tiled=True)  7.6 us
    dot_general x1, matrix products, back_project(): jnp.einsum('fcrx,focrs->fosx', masked, blocks, preferred_element_type=jnp...  3.96 us
  transfers between devices with their start and end apart: 2, of which 1 were waited for; matrix products, arithmetic and copies ran while one was open for 8% of the time, Pallas kernels for 0%

commit v1 on v0

--- a/solution.py
+++ b/solution.py
@@ -40,7 +40,10 @@
     freqs = freq_index.shape[0]
     cos_table = dft_table(freq_index, length)
     masked = green_rec * expand_map(block_map, receivers, green_rec.shape[3])[None, None]
-    regrouped = lax.all_to_all(traces, "freq", split_axis=2, concat_axis=0, tiled=True)
+    regrouped = jnp.concatenate(
+        lax.all_to_all(jnp.stack(jnp.split(traces, lax.axis_size("freq"), axis=2)), "freq", 0, 0),
+        axis=0,
+    )
     spectrum = transform(cos_table, regrouped, length).reshape(freqs, 2, receivers, shots // shards)
     gathered = lax.all_to_all(spectrum, "freq", split_axis=0, concat_axis=3, tiled=True)
     back_field = back_project(gathered, masked)

time: 168 us -> 192 us (1.14)
  local copies, waits for them, and re-layouts: 20.6 us -> 45.4 us
    split x0 -> x1, local copies, waits for them, and re-layouts: none -> 17.6 us  [body(): jnp.split(traces, lax.axis_size('freq'), axis=2)]
    unnamed x11 -> x25, local copies, waits for them, and re-layouts: 7.64 us -> 14 us
  transfers between devices with their start and end apart: 2 -> 2, of which waited for: 1 -> 1; matrix products, arithmetic and copies ran while one was open for 8% -> 7% of each run, Pallas kernels for 0% -> 0%
where the time goes in v1:
time: 192 us
  waiting for transfers between devices  77 us (40%)
  local copies, waits for them, and re-layouts  45.4 us (24%)
  blocking collectives  33.8 us (18%)
  starting transfers between devices  27.2 us (14%)
  matrix products  6.97 us (4%)
    all_to_all x1, waiting for transfers between devices, body(): lax.all_to_all(jnp.stack(jnp.split(traces, lax.axis_size('freq'), axis=2)...  77 us
    unnamed x1, blocking collectives  33.8 us
    all_to_all x1, starting transfers between devices, body(): lax.all_to_all(spectrum, 'freq', split_axis=0, concat_axis=3, tiled=True)  19.6 us
    split x1, local copies, waits for them, and re-layouts, body(): jnp.split(traces, lax.axis_size('freq'), axis=2)  17.6 us
    unnamed x25, local copies, waits for them, and re-layouts  14 us
    convert_element_type x3, local copies, waits for them, and re-layouts, expand_map(): jnp.repeat(jnp.repeat(block_map, row_span, axis=0), col_span, axis=1)  9.55 us
    all_to_all x1, starting transfers between devices, body(): lax.all_to_all(jnp.stack(jnp.split(traces, lax.axis_size('freq'), axis=2)...  7.6 us
    dot_general x1, matrix products, back_project(): jnp.einsum('fcrx,focrs->fosx', masked, blocks, preferred_element_type=jnp...  3.96 us
  transfers between devices with their start and end apart: 2, of which 1 were waited for; matrix products, arithmetic and copies ran while one was open for 7% of the time, Pallas kernels for 0%

profile of v1, /device:TPU:0, one launch (start us, length us, event | category | flops | bytes accessed | tf_op | source)
XLA Modules:
  0.0 191.7 jit_solution(3591067616009023110)
XLA Ops:
  0.0 17.6 %fusion.39 = (bf16[64,2048,1]{1,2,0:T(2,128)(2,1)S(1)}, bf16[64,2048,1]{1,2,0:T(2,128)(2,1)S(1)}, bf16[64,2048,1]{1,2,0:T(2,128)(2,1)S(1)}, bf16[64,2048,1]{1,2,...) fusion(bf16[64,2048,16]{1,2,0:T(8,128)(2,1)} %param.5), kind=kLoop, calls=%fused_computation.61 | loop fusion | bytes 8388608 | tf_op jit(solution)/shard_map/split | solution.py:44
  17.6 0.8 fusion.31
  18.4 0.9 fusion.30
  19.3 0.9 fusion.29
  20.1 0.9 fusion.28
  21.0 0.8 fusion.27
  21.9 0.9 fusion.26
  22.7 0.9 fusion.25
  23.6 0.8 fusion.24
  24.4 0.8 fusion.23
  25.3 0.9 fusion.22
  26.1 0.9 fusion.21
  27.0 0.9 fusion.20
  27.8 0.9 fusion.19
  28.7 0.8 fusion.18
  29.5 0.9 fusion.17
  30.4 0.9 fusion.16
  31.3 0.0 copy-start.2
  31.3 7.6 %all-to-all-start = ((bf16[16,64,2048,1]{2,1,3,0:T(8,128)(2,1)}), bf16[16,64,2048,1]{2,1,3,0:T(8,128)(2,1)}, u32[]{:S(2)}, u32[]{:S(2)}) async-start(bf16[16,64,2048,1]{2,1,3,0:T(8,128)(2,1)} %fusion.16), calls=%async_computation | async-start | bytes 8388608 | tf_op jit(solution)/shard_map/all_to_all | solution.py:44
  38.9 0.0 copy-done.2
  38.9 0.0 copy-start.1
  38.9 0.3 cosine_convert_fusion
  39.3 0.1 copy.100
  39.4 77.0 %all-to-all-done = bf16[16,64,2048,1]{2,1,3,0:T(8,128)(2,1)} async-done(((bf16[16,64,2048,1]{2,1,3,0:T(8,128)(2,1)}), bf16[16,64,2048,1]{2,1,3,0:T(8,128)(2,1)}, u32[]{:S(2)}, u32[]{:S(2)}) %all-to-all-start) | async-done | bytes 4194336 | tf_op jit(solution)/shard_map/all_to_all | solution.py:44
  116.4 3.0 %fusion.4 = bf16[32,2048]{1,0:T(8,128)(2,1)S(1)} fusion(bf16[32,1024]{1,0:T(8,128)(2,1)S(1)} %convert_element_type.47, bf16[1024,2048]{1,0:T(8,128)(2,1)} %bitcast.16), kind=kOutput, calls=%fused_computation.5 | convolution fusion | flops 134348800 | bytes 4390912 | tf_op jit(solution)/shard_map/dot_general | solution.py:25
  119.5 0.7 reshape.127
  120.2 19.6 %all-to-all-start.1 = ((bf16[16,2,2048,1]{2,1,3,0:T(2,128)(2,1)}), bf16[16,2,2048,1]{2,1,3,0:T(2,128)(2,1)S(1)}, u32[]{:S(2)}, u32[]{:S(2)}) async-start(bf16[16,2,2048,1]{2,1,3,0:T(2,128)(2,1)} %bitcast.17), calls=%async_computation.1 | async-start | bytes 262144 | tf_op jit(solution)/shard_map/all_to_all | solution.py:48
  139.9 0.0 copy-done.1
  139.9 0.1 broadcast_in_dim.4
  140.0 0.2 copy.119
  140.2 2.5 %broadcast_in_dim.10 = bf16[2048,64,12]{0,2,1:T(8,128)(2,1)} broadcast(bf16[2048,64]{0,1:T(8,128)(2,1)S(1)} %copy.119), dimensions={0,1} | broadcast | bytes 3407872 | tf_op jit(solution)/shard_map/broadcast_in_dim | solution.py:19
  142.6 6.2 %convert_element_type.51 = bf16[2048,768]{0,1:T(8,128)(2,1)} reshape(bf16[2048,64,12]{0,2,1:T(8,128)(2,1)} %broadcast_in_dim.10) | data formatting | bytes 6291456 | tf_op jit(solution)/shard_map/convert_element_type | solution.py:19
  148.8 0.0 copy-start.3
  148.8 0.0 copy-start
  148.8 3.2 %copy.120 = bf16[2048,768]{1,0:T(8,128)(2,1)S(1)} copy(bf16[2048,768]{0,1:T(8,128)(2,1)} %convert_element_type.51) | data formatting | bytes 6291456 | tf_op jit(solution)/shard_map/convert_element_type | solution.py:19
  152.0 0.0 copy-done.3
  152.0 0.6 dynamic-slice
  153.3 0.0 all-to-all-done.1
  153.4 0.0 copy-done
  153.4 4.0 %fusion.11 = f32[768]{0:T(1024)S(1)} fusion(bf16[1,2,2048,768]{3,2,1,0:T(8,128)(2,1)} %param.8, bf16[2048,768]{1,0:T(8,128)(2,1)S(1)} %copy.120, bf16[1,1,2,2048,16]{3,4,2,1,0:T(8,128)(2,1)S(1)} %maximum_bitcast_fusion.2, bf16[1,1,2,2048,16]{3,4,2,1,0:T(8,128)(2,1)S(1)} %bitcast.107, bf16[1,2,16,768]{3,2,1,0:T(8,128)(2,1)S(1)} %copy-done), kind=kOutput, calls=%fused_computation.8 | convolution fusion | flops 204676352 | bytes 9751552 | tf_op jit(solution)/shard_map/fcrx,focrs->fosx/dot_general | solution.py:32
  157.3 33.8 %all-reduce = f32[768]{0:T(1024)S(1)} all-reduce(f32[768]{0:T(1024)S(1)} %fusion.11), channel_id=2, replica_groups=mesh['groups'=2,'freq'=16] {'freq'}, use_global_device_ids=true, to_apply=%region_1.2.clone | all-reduce | flops 768 | bytes 6144
  191.2 0.6 dynamic-slice.1
  (6 shorter events, 0.1 us)
Async XLA Ops:
  31.3 7.6 %copy-start.2 = (s32[16]{0:T(128)S(1)}, s32[16]{0:T(128)}, u32[]{:S(2)}) copy-start(s32[16]{0:T(128)} %param.6) | copy-start | bytes 196
  31.3 85.1 %all-to-all-start = ((bf16[16,64,2048,1]{2,1,3,0:T(8,128)(2,1)}), bf16[16,64,2048,1]{2,1,3,0:T(8,128)(2,1)}, u32[]{:S(2)}, u32[]{:S(2)}) async-start(bf16[16,64,2048,1]{2,1,3,0:T(8,128)(2,1)} %fusion.16), calls=%async_computation | async-start | bytes 8388608 | tf_op jit(solution)/shard_map/all_to_all | solution.py:44
  38.9 101.0 %copy-start.1 = (s32[64,64]{1,0:T(8,128)S(1)}, s32[64,64]{1,0:T(8,128)}, u32[]{:S(2)}) copy-start(s32[64,64]{1,0:T(8,128)} %param.7) | copy-start | bytes 49156
  120.2 33.0 %all-to-all-start.1 = ((bf16[16,2,2048,1]{2,1,3,0:T(2,128)(2,1)}), bf16[16,2,2048,1]{2,1,3,0:T(2,128)(2,1)S(1)}, u32[]{:S(2)}, u32[]{:S(2)}) async-start(bf16[16,2,2048,1]{2,1,3,0:T(2,128)(2,1)} %bitcast.17), calls=%async_computation.1 | async-start | bytes 262144 | tf_op jit(solution)/shard_map/all_to_all | solution.py:48
  148.8 3.2 %copy-start.3 = (u32[32]{0:T(128)S(1)}, u32[32]{0:T(128)}, u32[]{:S(2)}) copy-start(u32[32]{0:T(128)} %constant.25) | copy-start | bytes 388
  148.8 4.6 %copy-start = (bf16[1,2,16,768]{3,2,1,0:T(8,128)(2,1)S(1)}, bf16[1,2,16,768]{3,2,1,0:T(8,128)(2,1)}, u32[]{:S(2)}) copy-start(bf16[1,2,16,768]{3,2,1,0:T(8,128)(2,1)} %param.9) | copy-start | bytes 147460
